TPU v7x, 32 devices: a 4x4x1 block of a 4x4x8 slice. The times are simulated.
32 devices in a mesh: rep: 2 (over z, core), dp: 16 (over x, y).
Axes of the slice: x: 4, y: 4, z: 1, core: 2. Of those that a mesh axis runs over, the one named last changes fastest.
The devices are a block of a 4x4x8 slice.
Arguments:
- a: bfloat16 [32, 4, 4096, 640], P(('rep', 'dp')), parts along dimension 0
- g: bfloat16 [32, 4, 4096, 2048], P(('rep', 'dp')), parts along dimension 0
Outputs:
- output: bfloat16 [8, 640, 2048], P('rep'), parts along dimension 0
There are 2 independent parts. A program takes and returns all parts, laid end to end along the dimension named above; each array names one.
All inputs are finite; a program needn't handle non-finite values.
Results may differ from a plain program's by a relative error of at most 0.012.
Values are sent between devices in bfloat16 or wider.
A program may use at most 768 MiB of HBM per device.

v0:
```python
import jax
import jax.numpy as jnp


def solution(mesh):
    groups = mesh.shape["rep"]

    def step(a, g):
        a, g = (t.reshape(groups, -1, *t.shape[1:]) for t in (a, g))
        sums = jnp.einsum("rsntd,rsntf->rndf", a, g, preferred_element_type=jnp.float32)
        return sums.astype(jnp.bfloat16).reshape(-1, *sums.shape[2:])

    return step
```

profile of v0, /device:TPU:97, one launch (start us, length us, event | category | flops | bytes accessed | tf_op | source)
XLA Modules:
  0.0 507.1 jit_solution(11417280993749959221)
XLA Ops:
  0.0 52.4 %fusion.3 = f32[1,4,640,2048]{3,2,1,0:T(8,128)} fusion(bf16[1,4,4096,2048]{3,2,1,0:T(8,128)(2,1)} %param.1, bf16[1,4,4096,640]{3,2,1,0:T(8,128)(2,1)} %param), kind=kOutput, calls=%fused_computation.4 | convolution fusion | flops 42949672960 | bytes 109051904 | tf_op jit(solution)/rsntd,rsntf->rndf/dot_general | solution.py:10
  52.4 454.7 %all-reduce.2 = bf16[1,4,640,2048]{3,2,1,0:T(8,128)(2,1)} all-reduce(f32[1,4,640,2048]{3,2,1,0:T(8,128)} %fusion.3), channel_id=1, replica_groups=[2,16]<=[32], use_global_device_ids=true, to_apply=%add.clone | all-reduce | flops 5242880 | bytes 31457280 | tf_op jit(solution)/rsntd,rsntf->rndf/dot_general | solution.py:10
where the time goes:
time: 507 us
  blocking collectives  455 us (90%)
  matrix products  52.4 us (10%)
    dot_general x1, blocking collectives, step(): jnp.einsum('rsntd,rsntf->rndf', a, g, preferred_element_type=jnp.float32)  455 us
    dot_general x1, matrix products, step(): jnp.einsum('rsntd,rsntf->rndf', a, g, preferred_element_type=jnp.float32)  52.4 us

commit v1 on v0

v1 whole, which is shorter than its diff:
```python
import functools
import math

import jax
import jax.numpy as jnp
from jax import lax
from jax.experimental import pallas as pl
from jax.experimental.pallas import tpu as pltpu
from jax.sharding import PartitionSpec as P

MESH = pl.DeviceIdType.MESH
F32, BF16 = jnp.float32, jnp.bfloat16
LANES = 128
GBUFS = 3
COMBINE1, OWN1, COMBINE2, OWN2, PASS2, SEND1 = 2, 4, 6, 8, 10, 12
PASS1, DONE1 = 2, 4


def kernel(side, chunks_per, a_ref, g_ref, out_ref, abuf, gbuf, acc, own, send1, recv1, part2, send2, recv2, obuf,
           asem, gsem, osem, ssem, rsem):
    mats, tokens, d = a_ref.shape
    chunks = mats * chunks_per
    half = d // 2
    quarter = half // side
    width = side * LANES
    strip = g_ref.shape[2] // side
    me = lax.axis_index("dp")
    pos = (me // side, lax.rem(me, side))
    core = lax.rem(lax.axis_index("rep"), 2)

    def device(axis, index):
        return {"dp": index * side + pos[1] if axis == 0 else pos[0] * side + index}

    def wrap(i):
        return lax.rem(i, side)

    def block(i, size):
        return pl.ds(pl.multiple_of(i * size, size), size)

    def parity(c):
        return lax.rem(c + core, 2)

    def to(axis, index, src, dst, kind, h, c):
        return pltpu.make_async_remote_copy(
            src_ref=src, dst_ref=dst, send_sem=ssem.at[kind, h, c], recv_sem=rsem.at[kind, h, c],
            device_id=device(axis, index), device_id_type=MESH)

    def copy_a(n):
        i = lax.rem(n, 2)
        return pltpu.make_async_copy(a_ref.at[n], abuf.at[i], asem.at[i])

    def copy_g(t, b):
        n, j, i = t // chunks_per, lax.rem(t, chunks_per), lax.rem(t, GBUFS)
        cols = pl.ds(pl.multiple_of(b * strip + j * LANES, LANES), LANES)
        return pltpu.make_async_copy(g_ref.at[n, :, cols], gbuf.at[i, :, pl.ds(b * LANES, LANES)], gsem.at[i])

    def whole_g(t):
        i = lax.rem(t, GBUFS)
        return pltpu.make_async_copy(g_ref.at[0, :, pl.ds(0, width)], gbuf.at[i], gsem.at[i])

    def start_g(t):
        for b in range(side):
            copy_g(t, b).start()

    def hop1(kind, h, c):
        p, s = pos[h], 1 + 2 * parity(c)
        index = wrap(p + s) if kind == 1 else wrap(p + side - s)
        return to(h, index, send1.at[kind, h, c], recv1.at[kind, h, c], kind, h, c)

    def matmul(t):
        n = t // chunks_per
        acc[...] = lax.dot_general(abuf[lax.rem(n, 2)], gbuf[lax.rem(t, GBUFS)], (((0,), (0,)), ((), ())),
                                   preferred_element_type=F32)
        r = lax.rem(t, OWN1)
        for h in range(2):
            rows = pl.ds(h * half, half)
            p, s = pos[h], 1 + 2 * parity(t)
            send1[0, h, t] = acc[rows, block(wrap(p + 2), LANES)].astype(BF16)
            send1[1, h, t] = acc[rows, block(wrap(p + s), LANES)].astype(BF16)
            own[r, h, 0] = acc[rows, block(wrap(p + side - s), LANES)]
            own[r, h, 1] = acc[rows, block(p, LANES)]

    def start1(t):
        for h in range(2):
            hop1(0, h, t).start()
            hop1(1, h, t).start()

    def combine1(c):
        r = lax.rem(c, OWN1)
        for h in range(2):
            hop1(0, h, c).wait_recv()
            send1[2, h, c] = (own[r, h, 0] + recv1[0, h, c].astype(F32)).astype(BF16)
            hop1(2, h, c).start()

    def hop2(kind, h, c):
        q, s = pos[1 - h], 1 + 2 * parity(c)
        index = wrap(q + s) if kind == 1 else wrap(q + side - s)
        return to(1 - h, index, send2.at[kind, h, c], recv2.at[kind, h, c], 3 + kind, h, c)

    def own1(c):
        r, r2 = lax.rem(c, OWN1), lax.rem(c, OWN2 - OWN1)
        for h in range(2):
            q, s = pos[1 - h], 1 + 2 * parity(c)
            hop1(1, h, c).wait_recv()
            hop1(2, h, c).wait_recv()
            part2[r2, h] = own[r, h, 1] + recv1[1, h, c].astype(F32) + recv1[2, h, c].astype(F32)
            send2[0, h, c] = part2[r2, h, block(wrap(q + 2), quarter)].astype(BF16)
            send2[1, h, c] = part2[r2, h, block(wrap(q + s), quarter)].astype(BF16)
            hop2(0, h, c).start()
            hop2(1, h, c).start()

    def combine2(c):
        r2 = lax.rem(c, OWN2 - OWN1)
        for h in range(2):
            q, s = pos[1 - h], 1 + 2 * parity(c)
            hop2(0, h, c).wait_recv()
            mine = part2[r2, h, block(wrap(q + side - s), quarter)]
            send2[2, h, c] = (mine + recv2[0, h, c].astype(F32)).astype(BF16)
            hop2(2, h, c).start()

    def columns(b, c):
        return pl.ds(pl.multiple_of(b * strip + lax.rem(c, chunks_per) * LANES, LANES), LANES)

    def gather2(kind, h, c):
        q, s = pos[1 - h], 1 + 2 * parity(c)
        owner = wrap(q + side - s) if kind == 2 else q
        index = wrap(q + (1, side - 1, s)[kind])
        rows = pl.ds(pl.multiple_of(h * half + owner * quarter, 16), quarter)
        ref = obuf.at[c // chunks_per, rows, columns(pos[h], c)]
        return to(1 - h, index, ref, ref, 6 + kind, h, c)

    def wait2(kind, h, c):
        ref = obuf.at[c // chunks_per, pl.ds(h * half, quarter), columns(pos[h], c)]
        pltpu.make_async_remote_copy(src_ref=ref, dst_ref=ref, send_sem=ssem.at[6, h, c], recv_sem=rsem.at[6 + kind, h, c],
                                     device_id=device(0, pos[0]), device_id_type=MESH).wait_recv()

    def own2(c):
        r2 = lax.rem(c, OWN2 - OWN1)
        for h in range(2):
            q = pos[1 - h]
            hop2(1, h, c).wait_recv()
            hop2(2, h, c).wait_recv()
            total = part2[r2, h, block(q, quarter)] + recv2[1, h, c].astype(F32) + recv2[2, h, c].astype(F32)
            rows = pl.ds(pl.multiple_of(h * half + q * quarter, 16), quarter)
            obuf[c // chunks_per, rows, columns(pos[h], c)] = total.astype(BF16)
            gather2(0, h, c).start()
            gather2(1, h, c).start()

    def pass2(c):
        for h in range(2):
            wait2(parity(c), h, c)
            gather2(2, h, c).start()

    def gather1(kind, h, c):
        p, s = pos[h], 1 + 2 * parity(c)
        owner = wrap(p + side - s) if kind == 2 else p
        index = wrap(p + (1, side - 1, s)[kind])
        ref = obuf.at[c // chunks_per, pl.ds(h * half, half), columns(owner, c)]
        return to(h, index, ref, ref, 9 + kind, h, c)

    def wait1(kind, h, c):
        ref = obuf.at[c // chunks_per, pl.ds(h * half, half), columns(pos[h], c)]
        pltpu.make_async_remote_copy(src_ref=ref, dst_ref=ref, send_sem=ssem.at[9, h, c], recv_sem=rsem.at[9 + kind, h, c],
                                     device_id=device(0, pos[0]), device_id_type=MESH).wait_recv()

    def send_whole(c):
        for h in range(2):
            wait2(1 - parity(c), h, c)
            wait2(2, h, c)
            gather1(0, h, c).start()
            gather1(1, h, c).start()

    def pass1(c):
        for h in range(2):
            wait1(parity(c), h, c)
            gather1(2, h, c).start()

    def copy_out(b, c):
        ref = (c // chunks_per, slice(None), columns(b, c))
        return pltpu.make_async_copy(obuf.at[ref], out_ref.at[ref], osem.at[b, c])

    def done1(c):
        for h in range(2):
            wait1(1 - parity(c), h, c)
            wait1(2, h, c)
        for b in range(side):
            copy_out(b, c).start()

    def when(step, c, last):
        @pl.when((c >= 0) & (c < last))
        def _():
            step(c)

    def reduce_steps(t):
        for step, lag in ((pass2, PASS2), (own2, OWN2), (combine2, COMBINE2), (own1, OWN1), (combine1, COMBINE1)):
            when(step, t - lag, chunks)

    barrier = pltpu.get_barrier_semaphore()
    neighbours = [device(axis, wrap(pos[axis] + k)) for axis in range(2) for k in (1, side - 1)]
    for nb in neighbours:
        pl.semaphore_signal(barrier, inc=1, device_id=nb, device_id_type=MESH)
    copy_a(0).start()
    for t in range(GBUFS - 1):
        start_g(t)

    start_g(GBUFS - 1)
    copy_a(0).wait()
    copy_a(1).start()
    whole_g(0).wait()
    matmul(0)
    pl.semaphore_wait(barrier, len(neighbours))
    start1(0)

    def compute_slot(t, carry):
        reduce_steps(t)

        @pl.when(t + GBUFS - 1 < chunks)
        def _():
            start_g(t + GBUFS - 1)

        @pl.when(lax.rem(t, chunks_per) == 0)
        def _():
            n = t // chunks_per

            @pl.when(n + 1 < mats)
            def _():
                copy_a(n + 1).start()

            copy_a(n).wait()

        whole_g(t).wait()
        matmul(t)
        start1(t)
        return carry

    lax.fori_loop(1, chunks, compute_slot, 0)

    def gather_slot(u, carry):
        reduce_steps(chunks + u)
        when(send_whole, u, chunks)
        when(pass1, u - PASS1, chunks)
        when(done1, u - DONE1, chunks)
        return carry

    lax.fori_loop(0, chunks + DONE1, gather_slot, 0)

    def finish(c, carry):
        for h in range(2):
            for kind in range(3):
                hop1(kind, h, c).wait_send()
                hop2(kind, h, c).wait_send()
                gather2(kind, h, c).wait_send()
                gather1(kind, h, c).wait_send()
        for b in range(side):
            copy_out(b, c).wait()
        return carry

    lax.fori_loop(0, chunks, finish, 0)


def solution(mesh):
    side = math.isqrt(mesh.shape["dp"])

    def local(a, g):
        _, mats, tokens, d = a.shape
        ff = g.shape[3]
        width = side * LANES
        chunks_per = ff // width
        chunks = mats * chunks_per
        half = d // 2
        quarter = half // side
        dma = pltpu.SemaphoreType.DMA
        return pl.pallas_call(
            functools.partial(kernel, side, chunks_per),
            out_shape=jax.ShapeDtypeStruct((mats, d, ff), BF16),
            in_specs=[pl.BlockSpec(memory_space=pltpu.HBM)] * 2,
            out_specs=pl.BlockSpec(memory_space=pltpu.HBM),
            scratch_shapes=[
                pltpu.VMEM((2, tokens, d), BF16),
                pltpu.VMEM((GBUFS, tokens, width), BF16),
                pltpu.VMEM((d, width), F32),
                pltpu.VMEM((OWN1, 2, 2, half, LANES), F32),
                pltpu.VMEM((3, 2, chunks, half, LANES), BF16),
                pltpu.VMEM((3, 2, chunks, half, LANES), BF16),
                pltpu.VMEM((OWN2 - OWN1, 2, half, LANES), F32),
                pltpu.VMEM((3, 2, chunks, quarter, LANES), BF16),
                pltpu.VMEM((3, 2, chunks, quarter, LANES), BF16),
                pltpu.VMEM((mats, d, ff), BF16),
                dma((2,)),
                dma((GBUFS,)),
                dma((side, chunks)),
                dma((12, 2, chunks)),
                dma((12, 2, chunks)),
            ],
            compiler_params=pltpu.CompilerParams(collective_id=0, has_side_effects=True, vmem_limit_bytes=65_000_000),
            cost_estimate=pl.CostEstimate(flops=2 * mats * tokens * d * ff, bytes_accessed=2 * mats * tokens * (d + ff),
                                          transcendentals=0),
            name="weight_gradients",
        )(a[0], g[0])

    return jax.shard_map(local, mesh=mesh, in_specs=(P(("rep", "dp")), P(("rep", "dp"))), out_specs=P("rep"), check_vma=False)
```

time: 507 us -> 148 us (0.29)
  blocking collectives: 455 us -> 0 us
  Pallas kernels: 0 us -> 137 us
  matrix products: 52.4 us -> 0 us
  local copies, waits for them, and re-layouts: 0 us -> 10.3 us
    dot_general x1 -> x0, blocking collectives: 455 us -> none  [step(): jnp.einsum('rsntd,rsntf->rndf', a, g, preferred_element_type=jnp.float32)]
    pallas_call x0 -> x1, Pallas kernels: none -> 137 us  [local(): pl.pallas_call(functools.partial(kernel, side, chunks_per), out_shape=jax...]
    dot_general x1 -> x0, matrix products: 52.4 us -> none  [step(): jnp.einsum('rsntd,rsntf->rndf', a, g, preferred_element_type=jnp.float32)]
    unnamed x0 -> x1, local copies, waits for them, and re-layouts: none -> 10.3 us
where the time goes in v1:
time: 148 us; the launch traced here: 147 us
  Pallas kernels  137 us (93%)
  local copies, waits for them, and re-layouts  10.3 us (7%)
    pallas_call x1, Pallas kernels, local(): pl.pallas_call(functools.partial(kernel, side, chunks_per), out_shape=jax...  137 us
    unnamed x1, local copies, waits for them, and re-layouts  10.3 us

profile of v1, /device:TPU:97, one launch (start us, length us, event | category | flops | bytes accessed | tf_op | source)
XLA Modules:
  0.0 147.2 jit_solution(16126563949821655426)
XLA Ops:
  0.0 136.9 %weight_gradients.1 = bf16[4,640,2048]{2,1,0:T(8,128)(2,1)} custom-call(bf16[4,4096,640]{2,1,0:T(8,128)(2,1)} %bitcast.2, bf16[4,4096,2048]{2,1,0:T(8,128)(2,1)} %bitcast.1.g_ref), custom_call_target="tpu_custom_call" | custom-call | flops 42949672960 | bytes 88080384 | tf_op jit(solution)/shard_map/weight_gradients/pallas_call | solution.py:273
  136.9 10.3 %copy.4 = bf16[4,640,2048]{2,1,0:T(8,128)(2,1)} copy(bf16[4,640,2048]{2,1,0:T(8,128)(2,1)} %weight_gradients.1) | data formatting | bytes 20971520

commit v2 on v0

v2 whole, which is shorter than its diff:
```python
import functools
import math

import jax
import jax.numpy as jnp
from jax import lax
from jax.experimental import pallas as pl
from jax.experimental.pallas import tpu as pltpu
from jax.sharding import PartitionSpec as P

MESH = pl.DeviceIdType.MESH
F32, BF16 = jnp.float32, jnp.bfloat16
LANES = 128
GBUFS = 3
GROUP = 2
HEAD = 4
COMBINE1, OWN1, COMBINE2, OWN2, PASS2 = 3, 6, 8, 10, 12
SEND1, PASS1, DONE1 = 16, 3, 6
OWN_RING = OWN1 + GROUP - 1
PART_RING = -(-(OWN2 - OWN1) // GROUP)


def kernel(side, chunks_per, a_ref, g_ref, out, abuf, gbuf, acc, own, send1, recv1, part2, send2, recv2,
           asem, gsem, hsem, ssem, rsem1, rsem2):
    mats, tokens, d = a_ref.shape
    chunks = mats * chunks_per
    groups = chunks // GROUP
    half = d // 2
    quarter = half // side
    width = side * LANES
    strip = g_ref.shape[2] // side
    me = lax.axis_index("dp")
    pos = (me // side, lax.rem(me, side))
    core = lax.rem(lax.axis_index("rep"), 2)

    def device(axis, index):
        return {"dp": index * side + pos[1] if axis == 0 else pos[0] * side + index}

    def wrap(i):
        return lax.rem(i, side)

    def block(i, size):
        return pl.ds(pl.multiple_of(i * size, size), size)

    def parity(c):
        return lax.rem(c + core, 2)

    def step(c):
        return 1 + 2 * parity(c)

    def to(axis, index, src, dst, send_sem, recv_sem):
        return pltpu.make_async_remote_copy(src_ref=src, dst_ref=dst, send_sem=send_sem, recv_sem=recv_sem,
                                            device_id=device(axis, index), device_id_type=MESH)

    def copy_a(n):
        i = lax.rem(n, 2)
        return pltpu.make_async_copy(a_ref.at[n], abuf.at[i], asem.at[i])

    def start_g(t):
        n, j, i = t // chunks_per, lax.rem(t, chunks_per), lax.rem(t, GBUFS)
        for b in range(side):
            cols = pl.ds(pl.multiple_of(b * strip + j * LANES, LANES), LANES)
            pltpu.make_async_copy(g_ref.at[n, :, cols], gbuf.at[i, :, pl.ds(b * LANES, LANES)], gsem.at[i]).start()

    def whole_g(t):
        i = lax.rem(t, GBUFS)
        return pltpu.make_async_copy(g_ref.at[0, :, pl.ds(0, width)], gbuf.at[i], gsem.at[i])

    def head_rows(k):
        return pl.ds(k * (tokens // HEAD), tokens // HEAD)

    def head_a(k):
        return pltpu.make_async_copy(a_ref.at[0, head_rows(k)], abuf.at[0, head_rows(k)], hsem.at[0, k])

    def start_head(k):
        head_a(k).start()
        for b in range(side):
            pltpu.make_async_copy(g_ref.at[0, head_rows(k), pl.ds(b * strip, LANES)],
                                  gbuf.at[0, head_rows(k), pl.ds(b * LANES, LANES)], hsem.at[1, k]).start()

    def wait_head(k):
        head_a(k).wait()
        pltpu.make_async_copy(g_ref.at[0, head_rows(k), pl.ds(0, width)], gbuf.at[0, head_rows(k)], hsem.at[1, k]).wait()

    def product(a, g):
        return lax.dot_general(a, g, (((0,), (0,)), ((), ())), preferred_element_type=F32)

    def hop1(kind, h, c):
        p, s = pos[h], step(c)
        index = wrap(p + s) if kind == 1 else wrap(p + side - s)
        return to(h, index, send1.at[kind, h, c], recv1.at[kind, h, c], ssem.at[0], rsem1.at[kind, h, c])

    def start1(t):
        r = lax.rem(t, OWN_RING)
        for h in range(2):
            rows = pl.ds(h * half, half)
            p, s = pos[h], step(t)
            send1[0, h, t] = acc[rows, block(wrap(p + 2), LANES)].astype(BF16)
            send1[1, h, t] = acc[rows, block(wrap(p + s), LANES)].astype(BF16)
            own[r, h, 0] = acc[rows, block(wrap(p + side - s), LANES)]
            own[r, h, 1] = acc[rows, block(p, LANES)]
        for h in range(2):
            hop1(0, h, t).start()
            hop1(1, h, t).start()

    def combine1(c):
        r = lax.rem(c, OWN_RING)
        for h in range(2):
            hop1(0, h, c).wait_recv()
            send1[2, h, c] = (own[r, h, 0] + recv1[0, h, c].astype(F32)).astype(BF16)
            hop1(2, h, c).start()

    def hop2(kind, h, k):
        q, s = pos[1 - h], step(k)
        index = wrap(q + s) if kind == 1 else wrap(q + side - s)
        return to(1 - h, index, send2.at[kind, h, k], recv2.at[kind, h, k], ssem.at[1], rsem2.at[kind, h, k])

    def own1(k):
        r2 = lax.rem(k, PART_RING)
        for h in range(2):
            q, s = pos[1 - h], step(k)
            for i in range(GROUP):
                c = k * GROUP + i
                hop1(1, h, c).wait_recv()
                hop1(2, h, c).wait_recv()
                part2[r2, h, i] = (own[lax.rem(c, OWN_RING), h, 1] + recv1[1, h, c].astype(F32)
                                   + recv1[2, h, c].astype(F32))
                send2[0, h, k, i] = part2[r2, h, i, block(wrap(q + 2), quarter)].astype(BF16)
                send2[1, h, k, i] = part2[r2, h, i, block(wrap(q + s), quarter)].astype(BF16)
            hop2(0, h, k).start()
            hop2(1, h, k).start()

    def combine2(k):
        r2 = lax.rem(k, PART_RING)
        for h in range(2):
            q, s = pos[1 - h], step(k)
            hop2(0, h, k).wait_recv()
            mine = part2[r2, h, :, block(wrap(q + side - s), quarter)]
            send2[2, h, k] = (mine + recv2[0, h, k].astype(F32)).astype(BF16)
            hop2(2, h, k).start()

    def columns(b, c, count):
        first = b * strip + lax.rem(c, chunks_per) * LANES
        return pl.ds(pl.multiple_of(first, count * LANES), count * LANES)

    def gather2(kind, h, k):
        q, s, c = pos[1 - h], step(k), k * GROUP
        owner = wrap(q + side - s) if kind == 2 else q
        index = wrap(q + (1, side - 1, s)[kind])
        rows = pl.ds(pl.multiple_of(h * half + owner * quarter, 16), quarter)
        ref = out.at[c // chunks_per, rows, columns(pos[h], c, GROUP)]
        return to(1 - h, index, ref, ref, ssem.at[2], rsem2.at[3 + kind, h, k])

    def wait2(kind, h, k):
        c = k * GROUP
        ref = out.at[c // chunks_per, pl.ds(h * half, quarter), columns(pos[h], c, GROUP)]
        to(h, pos[h], ref, ref, ssem.at[2], rsem2.at[3 + kind, h, k]).wait_recv()

    def own2(k):
        r2 = lax.rem(k, PART_RING)
        for h in range(2):
            q = pos[1 - h]
            hop2(1, h, k).wait_recv()
            hop2(2, h, k).wait_recv()
            rows = pl.ds(pl.multiple_of(h * half + q * quarter, 16), quarter)
            for i in range(GROUP):
                c = k * GROUP + i
                total = (part2[r2, h, i, block(q, quarter)] + recv2[1, h, k, i].astype(F32)
                         + recv2[2, h, k, i].astype(F32))
                out[c // chunks_per, rows, columns(pos[h], c, 1)] = total.astype(BF16)
            gather2(0, h, k).start()
            gather2(1, h, k).start()

    def pass2(k):
        for h in range(2):
            wait2(parity(k), h, k)
            gather2(2, h, k).start()

    def gather1(kind, h, k):
        p, s, c = pos[h], step(k), k * GROUP
        owner = wrap(p + side - s) if kind == 2 else p
        index = wrap(p + (1, side - 1, s)[kind])
        ref = out.at[c // chunks_per, pl.ds(h * half, half), columns(owner, c, GROUP)]
        return to(h, index, ref, ref, ssem.at[3], rsem2.at[6 + kind, h, k])

    def wait1(kind, h, k):
        c = k * GROUP
        ref = out.at[c // chunks_per, pl.ds(h * half, half), columns(pos[h], c, GROUP)]
        to(h, pos[h], ref, ref, ssem.at[3], rsem2.at[6 + kind, h, k]).wait_recv()

    def send_whole(k):
        for h in range(2):
            wait2(1 - parity(k), h, k)
            wait2(2, h, k)
            gather1(0, h, k).start()
            gather1(1, h, k).start()

    def pass1(k):
        for h in range(2):
            wait1(parity(k), h, k)
            gather1(2, h, k).start()

    def done1(k):
        for h in range(2):
            wait1(1 - parity(k), h, k)
            wait1(2, h, k)

    def per_chunk(do, c):
        @pl.when((c >= 0) & (c < chunks))
        def _():
            do(c)

    def per_group(do, c):
        k = c // GROUP

        @pl.when((c >= 0) & (k < groups) & (lax.rem(c, GROUP) == 0))
        def _():
            do(k)

    def steps(t):
        per_group(done1, t - SEND1 - DONE1)
        per_group(pass1, t - SEND1 - PASS1)
        per_group(send_whole, t - SEND1)
        per_group(pass2, t - PASS2 - GROUP + 1)
        per_group(own2, t - OWN2 - GROUP + 1)
        per_group(combine2, t - COMBINE2 - GROUP + 1)
        per_group(own1, t - OWN1 - GROUP + 1)
        per_chunk(combine1, t - COMBINE1)

    barrier = pltpu.get_barrier_semaphore()
    neighbours = [device(axis, wrap(pos[axis] + k)) for axis in range(2) for k in (1, side - 1)]
    for nb in neighbours:
        pl.semaphore_signal(barrier, inc=1, device_id=nb, device_id_type=MESH)
    for k in range(HEAD):
        start_head(k)
    for k in range(HEAD):
        wait_head(k)
        if k == 0:
            start_g(1)
        part = product(abuf[0, head_rows(k)], gbuf[0, head_rows(k)])
        acc[...] = part if k == 0 else acc[...] + part
    pl.semaphore_wait(barrier, len(neighbours))
    start1(0)
    start_g(2)
    copy_a(1).start()

    def compute_slot(t, carry):
        steps(t)

        @pl.when(t + GBUFS - 1 < chunks)
        def _():
            start_g(t + GBUFS - 1)

        @pl.when(lax.rem(t, chunks_per) == 0)
        def _():
            n = t // chunks_per

            @pl.when(n + 1 < mats)
            def _():
                copy_a(n + 1).start()

            copy_a(n).wait()

        whole_g(t).wait()
        acc[...] = product(abuf[lax.rem(t // chunks_per, 2)], gbuf[lax.rem(t, GBUFS)])
        start1(t)
        return carry

    lax.fori_loop(1, chunks, compute_slot, 0)

    def gather_slot(t, carry):
        steps(t)
        return carry

    lax.fori_loop(chunks, SEND1 + chunks - GROUP + DONE1 + 1, gather_slot, 0)

    to(0, pos[0], send1, recv1, ssem.at[0], rsem1.at[0, 0, 0]).wait_send()
    to(0, pos[0], send2, recv2, ssem.at[1], rsem2.at[0, 0, 0]).wait_send()
    to(0, pos[0], send2, recv2, ssem.at[2], rsem2.at[0, 0, 0]).wait_send()
    to(0, pos[0], send1, recv1, ssem.at[3], rsem2.at[0, 0, 0]).wait_send()


def solution(mesh):
    side = math.isqrt(mesh.shape["dp"])

    def local(a, g):
        _, mats, tokens, d = a.shape
        ff = g.shape[3]
        width = side * LANES
        chunks_per = ff // width
        chunks = mats * chunks_per
        groups = chunks // GROUP
        half = d // 2
        quarter = half // side
        dma = pltpu.SemaphoreType.DMA
        return pl.pallas_call(
            functools.partial(kernel, side, chunks_per),
            out_shape=pltpu.VMEM((mats, d, ff), BF16),
            in_specs=[pl.BlockSpec(memory_space=pltpu.HBM)] * 2,
            out_specs=pl.BlockSpec(memory_space=pltpu.VMEM),
            scratch_shapes=[
                pltpu.VMEM((2, tokens, d), BF16),
                pltpu.VMEM((GBUFS, tokens, width), BF16),
                pltpu.VMEM((d, width), F32),
                pltpu.VMEM((OWN_RING, 2, 2, half, LANES), F32),
                pltpu.VMEM((3, 2, chunks, half, LANES), BF16),
                pltpu.VMEM((3, 2, chunks, half, LANES), BF16),
                pltpu.VMEM((PART_RING, 2, GROUP, half, LANES), F32),
                pltpu.VMEM((3, 2, groups, GROUP, quarter, LANES), BF16),
                pltpu.VMEM((3, 2, groups, GROUP, quarter, LANES), BF16),
                dma((2,)),
                dma((GBUFS,)),
                dma((2, HEAD)),
                dma((4,)),
                dma((3, 2, chunks)),
                dma((9, 2, groups)),
            ],
            compiler_params=pltpu.CompilerParams(collective_id=0, has_side_effects=True, vmem_limit_bytes=55_000_000),
            cost_estimate=pl.CostEstimate(flops=2 * mats * tokens * d * ff, bytes_accessed=2 * mats * tokens * (d + ff),
                                          transcendentals=0),
            name="weight_gradients",
        )(a[0], g[0])

    return jax.shard_map(local, mesh=mesh, in_specs=(P(("rep", "dp")), P(("rep", "dp"))), out_specs=P("rep"), check_vma=False)
```

time: 507 us -> 132 us (0.26)
  blocking collectives: 455 us -> 0 us
  Pallas kernels: 0 us -> 128 us
  matrix products: 52.4 us -> 0 us
    dot_general x1 -> x0, blocking collectives: 455 us -> none  [step(): jnp.einsum('rsntd,rsntf->rndf', a, g, preferred_element_type=jnp.float32)]
    pallas_call x0 -> x1, Pallas kernels: none -> 128 us  [local(): pl.pallas_call(functools.partial(kernel, side, chunks_per), out_shape=plt...]
    dot_general x1 -> x0, matrix products: 52.4 us -> none  [step(): jnp.einsum('rsntd,rsntf->rndf', a, g, preferred_element_type=jnp.float32)]
where the time goes in v2:
time: 132 us
  Pallas kernels  128 us (97%)
  local copies, waits for them, and re-layouts  4.09 us (3%)
    pallas_call x1, Pallas kernels, local(): pl.pallas_call(functools.partial(kernel, side, chunks_per), out_shape=plt...  128 us
    unnamed x1, local copies, waits for them, and re-layouts  4.09 us

profile of v2, /device:TPU:97, one launch (start us, length us, event | category | flops | bytes accessed | tf_op | source)
XLA Modules:
  0.0 132.3 jit_solution(1212946730832095859)
XLA Ops:
  0.0 128.2 %weight_gradients.1 = bf16[4,640,2048]{2,1,0:T(8,128)(2,1)S(1)} custom-call(bf16[4,4096,640]{2,1,0:T(8,128)(2,1)} %bitcast.2, bf16[4,4096,2048]{2,1,0:T(8,128)(2,1)} %bitcast.1.g_ref), custom_call_target="tpu_custom_call" | custom-call | flops 42949672960 | bytes 88080384 | tf_op jit(solution)/shard_map/weight_gradients/pallas_call | solution.py:296
  128.2 4.1 %copy.4 = bf16[4,640,2048]{2,1,0:T(8,128)(2,1)} copy(bf16[4,640,2048]{2,1,0:T(8,128)(2,1)S(1)} %weight_gradients.1) | data formatting | bytes 20971520

commit v3 on v2

--- a/solution.py
+++ b/solution.py
@@ -14,11 +14,10 @@
 GBUFS = 3
 GROUP = 2
 HEAD = 4
-COMBINE1, OWN1, COMBINE2, OWN2, PASS2 = 3, 6, 8, 10, 12
-SEND1, PASS1, DONE1 = 16, 3, 6
-OWN_RING = OWN1 + GROUP - 1
-PART_RING = -(-(OWN2 - OWN1) // GROUP)
-
+COMBINE1, OWN1, COMBINE2, OWN2, PASS2 = 4, 8, 10, 14, 18
+SEND1, PASS1, DONE1 = 27, 9, 24
+OWN_RING = OWN1 // 2 + GROUP
+PART_RING = -(-(OWN2 - OWN1) // (2 * GROUP))
 
 def kernel(side, chunks_per, a_ref, g_ref, out, abuf, gbuf, acc, own, send1, recv1, part2, send2, recv2,
            asem, gsem, hsem, ssem, rsem1, rsem2):
@@ -28,6 +27,7 @@
     half = d // 2
     quarter = half // side
     width = side * LANES
+    cut = -(-half // LANES) * LANES
     strip = g_ref.shape[2] // side
     me = lax.axis_index("dp")
     pos = (me // side, lax.rem(me, side))
@@ -90,18 +90,16 @@
         index = wrap(p + s) if kind == 1 else wrap(p + side - s)
         return to(h, index, send1.at[kind, h, c], recv1.at[kind, h, c], ssem.at[0], rsem1.at[kind, h, c])
 
-    def start1(t):
+    def start1(h, t):
         r = lax.rem(t, OWN_RING)
-        for h in range(2):
-            rows = pl.ds(h * half, half)
-            p, s = pos[h], step(t)
-            send1[0, h, t] = acc[rows, block(wrap(p + 2), LANES)].astype(BF16)
-            send1[1, h, t] = acc[rows, block(wrap(p + s), LANES)].astype(BF16)
-            own[r, h, 0] = acc[rows, block(wrap(p + side - s), LANES)]
-            own[r, h, 1] = acc[rows, block(p, LANES)]
-        for h in range(2):
-            hop1(0, h, t).start()
-            hop1(1, h, t).start()
+        rows = pl.ds(h * half, half)
+        p, s = pos[h], step(t)
+        send1[0, h, t] = acc[rows, block(wrap(p + 2), LANES)].astype(BF16)
+        send1[1, h, t] = acc[rows, block(wrap(p + s), LANES)].astype(BF16)
+        own[r, h, 0] = acc[rows, block(wrap(p + side - s), LANES)]
+        own[r, h, 1] = acc[rows, block(p, LANES)]
+        hop1(0, h, t).start()
+        hop1(1, h, t).start()
 
     def combine1(c):
         r = lax.rem(c, OWN_RING)
@@ -205,27 +203,25 @@
             wait1(1 - parity(k), h, k)
             wait1(2, h, k)
 
-    def per_chunk(do, c):
-        @pl.when((c >= 0) & (c < chunks))
+    def at(do, t, now, first, every, count):
+        if (now - first) % 2:
+            return
+        late = 2 * t + now - first
+
+        @pl.when((late >= 0) & (late < every * count) & (lax.rem(late, every) == 0))
         def _():
-            do(c)
-
-    def per_group(do, c):
-        k = c // GROUP
-
-        @pl.when((c >= 0) & (k < groups) & (lax.rem(c, GROUP) == 0))
-        def _():
-            do(k)
-
-    def steps(t):
-        per_group(done1, t - SEND1 - DONE1)
-        per_group(pass1, t - SEND1 - PASS1)
-        per_group(send_whole, t - SEND1)
-        per_group(pass2, t - PASS2 - GROUP + 1)
-        per_group(own2, t - OWN2 - GROUP + 1)
-        per_group(combine2, t - COMBINE2 - GROUP + 1)
-        per_group(own1, t - OWN1 - GROUP + 1)
-        per_chunk(combine1, t - COMBINE1)
+            do(late // every)
+
+    def steps(t, now):
+        span, last = 2 * GROUP, 2 * GROUP - 1
+        at(done1, t, now, SEND1 + DONE1, span, groups)
+        at(pass1, t, now, SEND1 + PASS1, span, groups)
+        at(send_whole, t, now, SEND1, span, groups)
+        at(pass2, t, now, last + PASS2, span, groups)
+        at(own2, t, now, last + OWN2, span, groups)
+        at(combine2, t, now, last + COMBINE2, span, groups)
+        at(own1, t, now, last + OWN1, span, groups)
+        at(combine1, t, now, 1 + COMBINE1, 2, chunks)
 
     barrier = pltpu.get_barrier_semaphore()
     neighbours = [device(axis, wrap(pos[axis] + k)) for axis in range(2) for k in (1, side - 1)]
@@ -233,19 +229,23 @@
         pl.semaphore_signal(barrier, inc=1, device_id=nb, device_id_type=MESH)
     for k in range(HEAD):
         start_head(k)
+    upper = pl.ds(0, cut)
+    lower = pl.ds(cut, d - cut)
     for k in range(HEAD):
         wait_head(k)
         if k == 0:
             start_g(1)
-        part = product(abuf[0, head_rows(k)], gbuf[0, head_rows(k)])
-        acc[...] = part if k == 0 else acc[...] + part
+        part = product(abuf[0, head_rows(k), upper], gbuf[0, head_rows(k)])
+        acc[upper] = part if k == 0 else acc[upper] + part
     pl.semaphore_wait(barrier, len(neighbours))
-    start1(0)
+    start1(0, 0)
+    acc[lower] = product(abuf[0, :, lower], gbuf[0])
+    start1(1, 0)
     start_g(2)
     copy_a(1).start()
 
     def compute_slot(t, carry):
-        steps(t)
+        steps(t, 0)
 
         @pl.when(t + GBUFS - 1 < chunks)
         def _():
@@ -262,17 +262,23 @@
             copy_a(n).wait()
 
         whole_g(t).wait()
-        acc[...] = product(abuf[lax.rem(t // chunks_per, 2)], gbuf[lax.rem(t, GBUFS)])
-        start1(t)
+        i, j = lax.rem(t // chunks_per, 2), lax.rem(t, GBUFS)
+        acc[upper] = product(abuf[i, :, upper], gbuf[j])
+        steps(t, 1)
+        acc[lower] = product(abuf[i, :, lower], gbuf[j])
+        start1(0, t)
+        start1(1, t)
         return carry
 
     lax.fori_loop(1, chunks, compute_slot, 0)
 
     def gather_slot(t, carry):
-        steps(t)
+        steps(t, 0)
+        steps(t, 1)
         return carry
 
-    lax.fori_loop(chunks, SEND1 + chunks - GROUP + DONE1 + 1, gather_slot, 0)
+    end = SEND1 + DONE1 + 2 * (chunks - GROUP)
+    lax.fori_loop(chunks, end // 2 + 1, gather_slot, 0)
 
     to(0, pos[0], send1, recv1, ssem.at[0], rsem1.at[0, 0, 0]).wait_send()
     to(0, pos[0], send2, recv2, ssem.at[1], rsem2.at[0, 0, 0]).wait_send()

time: 132 us -> 130 us (0.985)
  Pallas kernels: 128 us -> 125 us
    pallas_call x1, Pallas kernels: 128 us -> 125 us  [local(): pl.pallas_call(functools.partial(kernel, side, chunks_per), out_shape=plt...]
where the time goes in v3:
time: 130 us; the launch traced here: 129 us
  Pallas kernels  125 us (96%)
  local copies, waits for them, and re-layouts  4.09 us (3%)
    pallas_call x1, Pallas kernels, local(): pl.pallas_call(functools.partial(kernel, side, chunks_per), out_shape=plt...  125 us
    unnamed x1, local copies, waits for them, and re-layouts  4.09 us

profile of v3, /device:TPU:97, one launch (start us, length us, event | category | flops | bytes accessed | tf_op | source)
XLA Modules:
  0.0 129.0 jit_solution(14602623227843588989)
XLA Ops:
  0.0 124.9 %weight_gradients.1 = bf16[4,640,2048]{2,1,0:T(8,128)(2,1)S(1)} custom-call(bf16[4,4096,640]{2,1,0:T(8,128)(2,1)} %bitcast.2, bf16[4,4096,2048]{2,1,0:T(8,128)(2,1)} %bitcast.1.g_ref), custom_call_target="tpu_custom_call" | custom-call | flops 42949672960 | bytes 88080384 | tf_op jit(solution)/shard_map/weight_gradients/pallas_call | solution.py:302
  124.9 4.1 %copy.4 = bf16[4,640,2048]{2,1,0:T(8,128)(2,1)} copy(bf16[4,640,2048]{2,1,0:T(8,128)(2,1)S(1)} %weight_gradients.1) | data formatting | bytes 20971520

commit v4 on v3

--- a/solution.py
+++ b/solution.py
@@ -14,12 +14,12 @@
 GBUFS = 3
 GROUP = 2
 HEAD = 4
-COMBINE1, OWN1, COMBINE2, OWN2, PASS2 = 4, 8, 10, 14, 18
+COMBINE1, OWN1, COMBINE2, OWN2, PASS2 = 4, 8, 11, 15, 19
 SEND1, PASS1, DONE1 = 27, 9, 24
-OWN_RING = OWN1 // 2 + GROUP
+ACC_RING = OWN1 // 2 + GROUP
 PART_RING = -(-(OWN2 - OWN1) // (2 * GROUP))
 
-def kernel(side, chunks_per, a_ref, g_ref, out, abuf, gbuf, acc, own, send1, recv1, part2, send2, recv2,
+def kernel(side, chunks_per, a_ref, g_ref, out, abuf, gbuf, acc, send1, recv1, part2, send2, recv2,
            asem, gsem, hsem, ssem, rsem1, rsem2):
     mats, tokens, d = a_ref.shape
     chunks = mats * chunks_per
@@ -70,7 +70,12 @@
         return pl.ds(k * (tokens // HEAD), tokens // HEAD)
 
     def head_a(k):
-        return pltpu.make_async_copy(a_ref.at[0, head_rows(k)], abuf.at[0, head_rows(k)], hsem.at[0, k])
+        part = (0, head_rows(k), pl.ds(0, cut))
+        return pltpu.make_async_copy(a_ref.at[part], abuf.at[part], hsem.at[0, k])
+
+    def rest_a():
+        part = (0, slice(None), pl.ds(cut, d - cut))
+        return pltpu.make_async_copy(a_ref.at[part], abuf.at[part], asem.at[0])
 
     def start_head(k):
         head_a(k).start()
@@ -90,22 +95,21 @@
         index = wrap(p + s) if kind == 1 else wrap(p + side - s)
         return to(h, index, send1.at[kind, h, c], recv1.at[kind, h, c], ssem.at[0], rsem1.at[kind, h, c])
 
+    def term(h, b, t):
+        return acc[lax.rem(t, ACC_RING), pl.ds(h * half, half), block(b, LANES)]
+
     def start1(h, t):
-        r = lax.rem(t, OWN_RING)
-        rows = pl.ds(h * half, half)
         p, s = pos[h], step(t)
-        send1[0, h, t] = acc[rows, block(wrap(p + 2), LANES)].astype(BF16)
-        send1[1, h, t] = acc[rows, block(wrap(p + s), LANES)].astype(BF16)
-        own[r, h, 0] = acc[rows, block(wrap(p + side - s), LANES)]
-        own[r, h, 1] = acc[rows, block(p, LANES)]
+        send1[0, h, t] = term(h, wrap(p + 2), t).astype(BF16)
+        send1[1, h, t] = term(h, wrap(p + s), t).astype(BF16)
         hop1(0, h, t).start()
         hop1(1, h, t).start()
 
     def combine1(c):
-        r = lax.rem(c, OWN_RING)
-        for h in range(2):
+        for h in range(2):
+            p, s = pos[h], step(c)
             hop1(0, h, c).wait_recv()
-            send1[2, h, c] = (own[r, h, 0] + recv1[0, h, c].astype(F32)).astype(BF16)
+            send1[2, h, c] = (term(h, wrap(p + side - s), c) + recv1[0, h, c].astype(F32)).astype(BF16)
             hop1(2, h, c).start()
 
     def hop2(kind, h, k):
@@ -121,8 +125,7 @@
                 c = k * GROUP + i
                 hop1(1, h, c).wait_recv()
                 hop1(2, h, c).wait_recv()
-                part2[r2, h, i] = (own[lax.rem(c, OWN_RING), h, 1] + recv1[1, h, c].astype(F32)
-                                   + recv1[2, h, c].astype(F32))
+                part2[r2, h, i] = term(h, pos[h], c) + recv1[1, h, c].astype(F32) + recv1[2, h, c].astype(F32)
                 send2[0, h, k, i] = part2[r2, h, i, block(wrap(q + 2), quarter)].astype(BF16)
                 send2[1, h, k, i] = part2[r2, h, i, block(wrap(q + s), quarter)].astype(BF16)
             hop2(0, h, k).start()
@@ -214,14 +217,14 @@
 
     def steps(t, now):
         span, last = 2 * GROUP, 2 * GROUP - 1
-        at(done1, t, now, SEND1 + DONE1, span, groups)
         at(pass1, t, now, SEND1 + PASS1, span, groups)
-        at(send_whole, t, now, SEND1, span, groups)
         at(pass2, t, now, last + PASS2, span, groups)
         at(own2, t, now, last + OWN2, span, groups)
         at(combine2, t, now, last + COMBINE2, span, groups)
         at(own1, t, now, last + OWN1, span, groups)
         at(combine1, t, now, 1 + COMBINE1, 2, chunks)
+        at(send_whole, t, now, SEND1, span, groups)
+        at(done1, t, now, SEND1 + DONE1, span, groups)
 
     barrier = pltpu.get_barrier_semaphore()
     neighbours = [device(axis, wrap(pos[axis] + k)) for axis in range(2) for k in (1, side - 1)]
@@ -229,6 +232,7 @@
         pl.semaphore_signal(barrier, inc=1, device_id=nb, device_id_type=MESH)
     for k in range(HEAD):
         start_head(k)
+    rest_a().start()
     upper = pl.ds(0, cut)
     lower = pl.ds(cut, d - cut)
     for k in range(HEAD):
@@ -236,10 +240,11 @@
         if k == 0:
             start_g(1)
         part = product(abuf[0, head_rows(k), upper], gbuf[0, head_rows(k)])
-        acc[upper] = part if k == 0 else acc[upper] + part
+        acc[0, upper] = part if k == 0 else acc[0, upper] + part
     pl.semaphore_wait(barrier, len(neighbours))
     start1(0, 0)
-    acc[lower] = product(abuf[0, :, lower], gbuf[0])
+    rest_a().wait()
+    acc[0, lower] = product(abuf[0, :, lower], gbuf[0])
     start1(1, 0)
     start_g(2)
     copy_a(1).start()
@@ -262,10 +267,10 @@
             copy_a(n).wait()
 
         whole_g(t).wait()
-        i, j = lax.rem(t // chunks_per, 2), lax.rem(t, GBUFS)
-        acc[upper] = product(abuf[i, :, upper], gbuf[j])
+        i, j, r = lax.rem(t // chunks_per, 2), lax.rem(t, GBUFS), lax.rem(t, ACC_RING)
+        acc[r, upper] = product(abuf[i, :, upper], gbuf[j])
         steps(t, 1)
-        acc[lower] = product(abuf[i, :, lower], gbuf[j])
+        acc[r, lower] = product(abuf[i, :, lower], gbuf[j])
         start1(0, t)
         start1(1, t)
         return carry
@@ -307,8 +312,7 @@
             scratch_shapes=[
                 pltpu.VMEM((2, tokens, d), BF16),
                 pltpu.VMEM((GBUFS, tokens, width), BF16),
-                pltpu.VMEM((d, width), F32),
-                pltpu.VMEM((OWN_RING, 2, 2, half, LANES), F32),
+                pltpu.VMEM((ACC_RING, d, width), F32),
                 pltpu.VMEM((3, 2, chunks, half, LANES), BF16),
                 pltpu.VMEM((3, 2, chunks, half, LANES), BF16),
                 pltpu.VMEM((PART_RING, 2, GROUP, half, LANES), F32),

time: 130 us -> 129 us (level)
  no operation moved by 1% of the time
where the time goes in v4:
time: 129 us
  Pallas kernels  125 us (97%)
  local copies, waits for them, and re-layouts  4.09 us (3%)
    pallas_call x1, Pallas kernels, local(): pl.pallas_call(functools.partial(kernel, side, chunks_per), out_shape=plt...  125 us
    unnamed x1, local copies, waits for them, and re-layouts  4.09 us

profile of v4, /device:TPU:97, one launch (start us, length us, event | category | flops | bytes accessed | tf_op | source)
XLA Modules:
  0.0 128.7 jit_solution(16958574538801434)
XLA Ops:
  0.0 124.6 %weight_gradients.1 = bf16[4,640,2048]{2,1,0:T(8,128)(2,1)S(1)} custom-call(bf16[4,4096,640]{2,1,0:T(8,128)(2,1)} %bitcast.2, bf16[4,4096,2048]{2,1,0:T(8,128)(2,1)} %bitcast.1.g_ref), custom_call_target="tpu_custom_call" | custom-call | flops 42949672960 | bytes 88080384 | tf_op jit(solution)/shard_map/weight_gradients/pallas_call | solution.py:307
  124.6 4.1 %copy.4 = bf16[4,640,2048]{2,1,0:T(8,128)(2,1)} copy(bf16[4,640,2048]{2,1,0:T(8,128)(2,1)S(1)} %weight_gradients.1) | data formatting | bytes 20971520

commit v5 on v4

--- a/solution.py
+++ b/solution.py
@@ -14,8 +14,8 @@
 GBUFS = 3
 GROUP = 2
 HEAD = 4
-COMBINE1, OWN1, COMBINE2, OWN2, PASS2 = 4, 8, 11, 15, 19
-SEND1, PASS1, DONE1 = 27, 9, 24
+COMBINE1, OWN1, COMBINE2, OWN2, PASS2 = 4, 8, 11, 14, 18
+SEND1, PASS1, DONE1 = 28, 9, 24
 ACC_RING = OWN1 // 2 + GROUP
 PART_RING = -(-(OWN2 - OWN1) // (2 * GROUP))
 
@@ -270,8 +270,8 @@
         i, j, r = lax.rem(t // chunks_per, 2), lax.rem(t, GBUFS), lax.rem(t, ACC_RING)
         acc[r, upper] = product(abuf[i, :, upper], gbuf[j])
         steps(t, 1)
+        start1(0, t)
         acc[r, lower] = product(abuf[i, :, lower], gbuf[j])
-        start1(0, t)
         start1(1, t)
         return carry
 

time: 129 us -> 129 us (level)
  no operation moved by 1% of the time
where the time goes in v5:
time: 129 us
  Pallas kernels  124 us (96%)
  local copies, waits for them, and re-layouts  4.09 us (3%)
    pallas_call x1, Pallas kernels, local(): pl.pallas_call(functools.partial(kernel, side, chunks_per), out_shape=plt...  124 us
    unnamed x1, local copies, waits for them, and re-layouts  4.09 us

profile of v5, /device:TPU:97, one launch (start us, length us, event | category | flops | bytes accessed | tf_op | source)
XLA Modules:
  0.0 128.6 jit_solution(4177092427698070522)
XLA Ops:
  0.0 124.5 %weight_gradients.1 = bf16[4,640,2048]{2,1,0:T(8,128)(2,1)S(1)} custom-call(bf16[4,4096,640]{2,1,0:T(8,128)(2,1)} %bitcast.2, bf16[4,4096,2048]{2,1,0:T(8,128)(2,1)} %bitcast.1.g_ref), custom_call_target="tpu_custom_call" | custom-call | flops 42949672960 | bytes 88080384 | tf_op jit(solution)/shard_map/weight_gradients/pallas_call | solution.py:307
  124.5 4.1 %copy.4 = bf16[4,640,2048]{2,1,0:T(8,128)(2,1)} copy(bf16[4,640,2048]{2,1,0:T(8,128)(2,1)S(1)} %weight_gradients.1) | data formatting | bytes 20971520
